TPU v7x, 32 devices: a whole 2x2x4 slice. The times are simulated.
32 devices in a mesh: groups: 2 (over y), expert: 16 (over z, x, core).
Axes of the slice: x: 2, y: 2, z: 4, core: 2. Of those that a mesh axis runs over, the one named last changes fastest.
Arguments:
- tokens: bfloat16 [512, 3584], P(('groups', 'expert')), parts along dimension 0, may hold values from -6 to 6
- live_counts: int32 [32], P(('groups', 'expert')), parts along dimension 0, may hold values from 8 to 16, as said below
- expert_ids: int32 [512, 4], P(('groups', 'expert')), parts along dimension 0, may hold values from 0 to 7, all different within a row; in each aligned block of 16 rows (0 to 15, 16 to 31, ...) at most 16 rows name the same one
- gate_scores: float32 [512, 4], P(('groups', 'expert')), parts along dimension 0, may hold values from 0.1 to 1
- gate_weight: bfloat16 [16, 3584, 512], P('expert'), may hold values from -0.09375 to 0.09375
- up_weight: bfloat16 [16, 3584, 512], P('expert'), may hold values from -0.09375 to 0.09375
- down_weight: bfloat16 [16, 512, 3584], P('expert'), may hold values from -0.1875 to 0.1875
Outputs:
- moe_out: bfloat16 [512, 3584], P(('groups', 'expert')), parts along dimension 0
There are 2 independent parts, one for each index of `groups`. A program takes and returns all parts, laid end to end along the dimension named above; an argument that names none is the same for every part. Nothing has to cross between parts.
Inputs may be any that keep to these rules, and one draw needn't show every extreme that they name: `expert_ids`: A row names 4 different experts. In each device's aligned block of 16 rows no expert is named by more than 16 rows, a bound that some block reaches. `live_counts`: some device has all 16 slots live.
All inputs are finite; a program needn't handle non-finite values.
Results may differ from a plain program's by a relative error of at most 0.0068.
Values may be sent and summed in bfloat16 or wider, within the bound.
A program may use at most 64 MiB of HBM per device.

v0:
```python
import jax
import jax.numpy as jnp
from jax import lax
from jax.sharding import PartitionSpec as P


def partner_2(block, axis, apart):
    count = lax.axis_size(axis)
    route = []
    for low in range(count):
        high = low | 1 << apart
        if high != low and high < count:
            route += [(low, high), (high, low)]
    return lax.ppermute(block, axis, route)


def expert_rows(slot_rows, gate_weight, up_weight, down_weight):
    model_width = slot_rows.shape[-1]
    flat_rows = slot_rows.reshape(-1, model_width)
    gate_act = jnp.dot(flat_rows, gate_weight[0], preferred_element_type=jnp.float32)
    up_act = jnp.dot(flat_rows, up_weight[0], preferred_element_type=jnp.float32)
    hidden = (jax.nn.silu(gate_act) * up_act).astype(jnp.bfloat16)
    partial_value = jnp.dot(hidden, down_weight[0], preferred_element_type=jnp.float32)
    return partial_value.reshape(slot_rows.shape)


def shards(tokens, live_counts, expert_ids, gate_scores, gate_weight, up_weight, down_weight):
    tok_dev, model_width = tokens.shape
    top_count = expert_ids.shape[1]
    devices = lax.axis_size("expert")
    experts = devices // 2
    capacity = 2 * tok_dev * top_count // experts
    half_width = model_width // 2
    parity = lax.axis_index("expert") % 2
    flat_ids = expert_ids.reshape(-1)
    onehot = (flat_ids[:, None] == jnp.arange(experts, dtype=jnp.int32)[None, :]).astype(jnp.int32)
    earlier = jnp.cumsum(onehot, axis=0) - onehot
    slot_index = jnp.sum(earlier * onehot, axis=1)
    target = flat_ids * capacity + slot_index
    placing = (jnp.arange(experts * capacity, dtype=jnp.int32)[:, None] == target[None, :]).astype(
        jnp.int32
    )
    placing = (
        placing.reshape(experts * capacity, tok_dev, top_count).sum(axis=2).astype(jnp.bfloat16)
    )
    packed = jnp.dot(placing, tokens, preferred_element_type=jnp.float32).astype(jnp.bfloat16)
    outgoing = packed.reshape(devices, capacity // 2, model_width)
    slot_rows = lax.all_to_all(outgoing, "expert", split_axis=0, concat_axis=0, tiled=True)
    partner = partner_2(slot_rows, "expert", 0)
    count = slot_rows.shape[1]
    run_slot_rows = jnp.concatenate([slot_rows, partner], axis=1)
    paired = expert_rows(run_slot_rows, gate_weight, up_weight, down_weight)
    own_part = paired[:, :count]
    partner_part = paired[:, count:]
    lower_half = jnp.where(parity == 0, own_part, partner_part)
    second = jnp.where(parity == 0, partner_part, own_part)
    stacked = jnp.stack([lower_half, second], axis=1)
    partial_value = stacked.reshape(devices, capacity, model_width)
    partner_sum = partner_2(partial_value, "expert", 0)
    summed = partial_value + partner_sum
    own_part = lax.dynamic_slice_in_dim(summed, parity * half_width, half_width, 2).astype(
        jnp.bfloat16
    )
    returned = lax.all_to_all(own_part, "expert", split_axis=0, concat_axis=0, tiled=True)
    returned = returned.reshape(experts, 2, capacity, half_width)
    picked = returned[flat_ids, :, slot_index, :]
    picked = picked.reshape(tok_dev, top_count, model_width).astype(jnp.float32)
    weighted = jnp.sum(picked * gate_scores[:, :, None], axis=1)
    live_mask = jnp.arange(tok_dev, dtype=jnp.int32) < live_counts[0]
    return jnp.where(live_mask[:, None], weighted, jnp.zeros_like(weighted)).astype(jnp.bfloat16)


def solution(mesh):
    in_specs = (
        P(("groups", "expert"), None),
        P(("groups", "expert")),
        P(("groups", "expert"), None),
        P(("groups", "expert"), None),
        P("expert", None, None),
        P("expert", None, None),
        P("expert", None, None),
    )
    out_specs = P(("groups", "expert"), None)
    return jax.shard_map(shards, mesh=mesh, in_specs=in_specs, out_specs=out_specs, check_vma=False)
```

profile of v0, /device:TPU:20, one launch (start us, length us, event | category | flops | bytes accessed | tf_op | source)
XLA Modules:
  0.0 82.1 jit_solution(15690689584253438499)
XLA Ops:
  0.0 0.8 copy.30
  0.8 0.1 eq.37
  0.9 0.1 fusion.8
  1.0 0.1 reduce_window_sum.11
  1.1 0.2 select_reduce_fusion
  1.2 0.1 reduce_sum.32
  1.3 0.1 copy.31
  1.4 0.7 multiply_add_fusion
  2.1 0.1 convert_reduce_fusion
  2.2 0.4 fusion
  2.6 28.2 %all_to_all.10 = bf16[16,8,3584]{2,1,0:T(8,128)(2,1)S(1)} all-to-all(bf16[16,8,3584]{2,1,0:T(8,128)(2,1)S(1)} %fusion), channel_id=1, replica_groups=mesh['groups'=2,'expert'=16] {'expert'}, dimensions={0} | all-to-all | bytes 1835008 | tf_op jit(solution)/shard_map/all_to_all | solution.py:48
  30.9 2.5 %collective-permute-done = bf16[16,8,3584]{2,1,0:T(8,128)(2,1)S(1)} collective-permute-done((bf16[16,8,3584]{2,1,0:T(8,128)(2,1)S(1)}, bf16[16,8,3584]{2,1,0:T(8,128)(2,1)S(1)}, u32[]{:S(2)}, u32[]{:S(2)}) %collective-permute-start) | collective-permute-done | bytes 917536 | tf_op jit(solution)/shard_map/ppermute | solution.py:14
  33.3 0.2 pad_maximum_fusion.1
  33.5 1.1 %fusion.5 = f32[256,512]{1,0:T(8,128)S(1)} fusion(bf16[256,3584]{1,0:T(8,128)(2,1)S(1)} %bitcast.36, bf16[1,3584,512]{2,1,0:T(8,128)(2,1)S(1)} %copy-done.3), kind=kOutput, calls=%fused_computation.8 | convolution fusion | flops 939524096 | bytes 6029312 | tf_op jit(solution)/shard_map/dot_general | solution.py:20
  34.7 0.9 %copy-done.4 = bf16[1,3584,512]{2,1,0:T(8,128)(2,1)S(1)} copy-done((bf16[1,3584,512]{2,1,0:T(8,128)(2,1)S(1)}, bf16[1,3584,512]{2,1,0:T(8,128)(2,1)}, u32[]{:S(2)}) %copy-start.4) | copy-done | bytes 3670040
  35.6 1.1 %multiply_convert_fusion = bf16[256,512]{1,0:T(8,128)(2,1)S(1)} fusion(f32[256,512]{1,0:T(8,128)S(1)} %fusion.5, bf16[256,3584]{1,0:T(8,128)(2,1)S(1)} %bitcast.37, bf16[1,3584,512]{2,1,0:T(8,128)(2,1)S(1)} %copy-done.4), kind=kOutput, calls=%fused_computation.17 | convolution fusion | flops 940310528 | bytes 6291456 | tf_op jit(solution)/shard_map/dot_general | solution.py:21
  36.7 0.9 %copy-done.1 = bf16[1,512,3584]{2,1,0:T(8,128)(2,1)S(1)} copy-done((bf16[1,512,3584]{2,1,0:T(8,128)(2,1)S(1)}, bf16[1,512,3584]{2,1,0:T(8,128)(2,1)}, u32[]{:S(2)}) %copy-start.1) | copy-done | bytes 3670040
  37.6 1.1 %fusion.1 = f32[16,16,3584]{2,1,0:T(8,128)S(1)} fusion(bf16[16,16,512]{2,1,0:T(8,128)(2,1)S(1)} %bitcast.38, bf16[1,512,3584]{2,1,0:T(8,128)(2,1)S(1)} %copy-done.1), kind=kOutput, calls=%fused_computation.4 | convolution fusion | flops 939524096 | bytes 7602176 | tf_op jit(solution)/shard_map/dot_general | solution.py:23
  38.7 0.3 select_bitcast_fusion.1
  39.0 2.1 %copy_bitcast_fusion = f32[16,16,3584]{2,1,0:T(8,128)} fusion(f32[16,1,8,3584]{3,2,0,1:T(8,128)S(1)} %get-tuple-element.6, f32[16,1,8,3584]{3,2,0,1:T(8,128)S(1)} %get-tuple-element.5), kind=kLoop, calls=%fused_computation.10 | loop fusion | flops 917504 | bytes 7340032 | tf_op jit(solution)/shard_map/reshape | solution.py:58
  41.1 0.1 collective-permute-start.1
  41.2 6.6 %collective-permute-done.1 = f32[16,16,3584]{2,1,0:T(8,128)} collective-permute-done((f32[16,16,3584]{2,1,0:T(8,128)}, f32[16,16,3584]{2,1,0:T(8,128)}, u32[]{:S(2)}, u32[]{:S(2)}) %collective-permute-start.1) | collective-permute-done | bytes 3670048 | tf_op jit(solution)/shard_map/ppermute | solution.py:14
  47.9 3.1 %fusion.7 = bf16[16,16,1792]{2,1,0:T(8,128)(2,1)} fusion(f32[16,16,3584]{2,1,0:T(8,128)} %collective-permute-done.1, s32[]{:T(128)S(6)} %select_n.50, f32[16,16,3584]{2,1,0:T(8,128)} %copy_bitcast_fusion), kind=kLoop, calls=%fused_computation.12 | loop fusion | flops 917504 | bytes 4587524 | tf_op jit(solution)/shard_map/convert_element_type | solution.py:61
  51.0 4.6 %all-to-all-start.1 = ((bf16[16,16,1792]{2,1,0:T(8,128)(2,1)}), bf16[16,16,1792]{2,1,0:T(8,128)(2,1)S(1)}, u32[]{:S(2)}, u32[]{:S(2)}) async-start(bf16[16,16,1792]{2,1,0:T(8,128)(2,1)} %fusion.7), calls=%async_computation.1 | async-start | bytes 1835008 | tf_op jit(solution)/shard_map/all_to_all | solution.py:64
  55.6 0.1 reshape.88
  55.7 0.1 copy.35
  56.5 21.5 %all-to-all-done.1 = bf16[16,16,1792]{2,1,0:T(8,128)(2,1)S(1)} async-done(((bf16[16,16,1792]{2,1,0:T(8,128)(2,1)}), bf16[16,16,1792]{2,1,0:T(8,128)(2,1)S(1)}, u32[]{:S(2)}, u32[]{:S(2)}) %all-to-all-start.1) | async-done | bytes 917536 | tf_op jit(solution)/shard_map/all_to_all | solution.py:64
  78.0 0.8 copy.34
  78.8 1.5 %gather_fusion = bf16[64,2,1792]{2,1,0:T(2,128)(2,1)S(1)} fusion(bf16[8,2,16,1792]{3,1,2,0:T(2,128)(2,1)S(1)} %copy.34, s32[64]{0:T(128)S(1)} %fusion.15), kind=kCustom, calls=%fused_computation | custom fusion | bytes 918016 | tf_op jit(solution)/shard_map/gather | solution.py:66
  80.3 0.4 reshape.89
  80.7 0.6 multiply_reduce_fusion
  81.4 0.7 select_convert_fusion
  (11 shorter events, 0.0 us)
Async XLA Ops:
  0.0 2.2 %copy-start = (bf16[16,3584]{1,0:T(8,128)(2,1)S(1)}, bf16[16,3584]{1,0:T(8,128)(2,1)}, u32[]{:S(2)}) copy-start(bf16[16,3584]{1,0:T(8,128)(2,1)} %param.7) | copy-start | bytes 344068
  30.9 2.5 %collective-permute-start = (bf16[16,8,3584]{2,1,0:T(8,128)(2,1)S(1)}, bf16[16,8,3584]{2,1,0:T(8,128)(2,1)S(1)}, u32[]{:S(2)}, u32[]{:S(2)}) collective-permute-start(bf16[16,8,3584]{2,1,0:T(8,128)(2,1)S(1)} %all_to_all.10), channel_id=1, source_target_pairs={{0,1},{1,0},{2,3},{3,2},{4,5},{5,4},{6,7},{7,6},{8,9},{9,8},{10,11... | collective-permute-start | bytes 2752520 | tf_op jit(solution)/shard_map/ppermute | solution.py:14
  30.9 2.7 %copy-start.3 = (bf16[1,3584,512]{2,1,0:T(8,128)(2,1)S(1)}, bf16[1,3584,512]{2,1,0:T(8,128)(2,1)}, u32[]{:S(2)}) copy-start(bf16[1,3584,512]{2,1,0:T(8,128)(2,1)} %param.11) | copy-start | bytes 11010052
  33.5 2.0 %copy-start.4 = (bf16[1,3584,512]{2,1,0:T(8,128)(2,1)S(1)}, bf16[1,3584,512]{2,1,0:T(8,128)(2,1)}, u32[]{:S(2)}) copy-start(bf16[1,3584,512]{2,1,0:T(8,128)(2,1)} %param.12) | copy-start | bytes 11010052
  35.6 2.0 %copy-start.1 = (bf16[1,512,3584]{2,1,0:T(8,128)(2,1)S(1)}, bf16[1,512,3584]{2,1,0:T(8,128)(2,1)}, u32[]{:S(2)}) copy-start(bf16[1,512,3584]{2,1,0:T(8,128)(2,1)} %param.13) | copy-start | bytes 11010052
  41.1 14.6 %copy-start.2 = (f32[16,4]{0,1:T(4,128)S(1)}, f32[16,4]{0,1:T(4,128)}, u32[]{:S(2)}) copy-start(f32[16,4]{0,1:T(4,128)} %param.10) | copy-start | bytes 772
  41.1 6.8 %collective-permute-start.1 = (f32[16,16,3584]{2,1,0:T(8,128)}, f32[16,16,3584]{2,1,0:T(8,128)}, u32[]{:S(2)}, u32[]{:S(2)}) collective-permute-start(f32[16,16,3584]{2,1,0:T(8,128)} %copy_bitcast_fusion), channel_id=1, source_target_pairs={{0,1},{1,0},{2,3},{3,2},{4,5},{5,4},{6,7},{7,6},{8,9},{9,8},{10,11... | collective-permute-start | bytes 11010056 | tf_op jit(solution)/shard_map/ppermute | solution.py:14
  51.0 27.0 %all-to-all-start.1 = ((bf16[16,16,1792]{2,1,0:T(8,128)(2,1)}), bf16[16,16,1792]{2,1,0:T(8,128)(2,1)S(1)}, u32[]{:S(2)}, u32[]{:S(2)}) async-start(bf16[16,16,1792]{2,1,0:T(8,128)(2,1)} %fusion.7), calls=%async_computation.1 | async-start | bytes 1835008 | tf_op jit(solution)/shard_map/all_to_all | solution.py:64
where the time goes:
time: 82.8 us; the launch traced here: 82.1 us
  waiting for transfers between devices  30.6 us (37%)
  blocking collectives  28.2 us (34%)
  other arithmetic  8.22 us (10%)
  local copies, waits for them, and re-layouts  5.76 us (7%)
  starting transfers between devices  4.78 us (6%)
  matrix products  3.75 us (5%)
    all_to_all x1, blocking collectives, shards(): lax.all_to_all(outgoing, 'expert', split_axis=0, concat_axis=0, tiled=True)  28.2 us
    all_to_all x1, waiting for transfers between devices, shards(): lax.all_to_all(own_part, 'expert', split_axis=0, concat_axis=0, tiled=True)  21.5 us
    ppermute x2, waiting for transfers between devices, partner_2(): return lax.ppermute(block, axis, route)  9.08 us
    all_to_all x1, starting transfers between devices, shards(): lax.all_to_all(own_part, 'expert', split_axis=0, concat_axis=0, tiled=True)  4.64 us
    convert_element_type x1, other arithmetic, shards(): lax.dynamic_slice_in_dim(summed, parity * half_width, half_width, 2)  3.15 us
    unnamed x12, local copies, waits for them, and re-layouts  2.72 us
    reshape x1, other arithmetic, shards(): partial_value = stacked.reshape(devices, capacity, model_width)  2.07 us
  transfers between devices with their start and end apart: 3, of which 3 were waited for; matrix products, arithmetic and copies ran while one was open for 0% of the time, Pallas kernels for 0%

commit v1 on v0

--- a/solution.py
+++ b/solution.py
@@ -1,7 +1,208 @@
+import functools
+
 import jax
 import jax.numpy as jnp
 from jax import lax
+from jax.experimental import pallas as pl
+from jax.experimental.pallas import tpu as pltpu
 from jax.sharding import PartitionSpec as P
+
+LANES = 128
+HALF = LANES // 2
+
+
+def flipped(value, mask):
+    bit = 1
+    while bit <= mask:
+        if mask & bit:
+            value = value + bit * (1 - 2 * ((value // bit) % 2))
+        bit *= 2
+    return value
+
+
+def dense_kernel(
+    planes, live_ref, tok_ref, ids_ref, score_ref, gate_hbm, up_hbm, down_hbm, out_ref,
+    held, w_gate, w_up, w_down, kept, to_pair, from_pair, to_side, from_side, to_far, from_far,
+    weight_sem, ag_send, ag_recv, pair_send, pair_recv, side_send, side_recv, far_send, far_recv,
+):
+    rows, width = tok_ref.shape
+    me = lax.axis_index("expert")
+    core, col, plane = me % 2, (me // 2) % 2, me // 4
+    place = [flipped(plane, i) for i in range(planes)]
+
+    def device(p, x, c):
+        return (p * 2 + x) * 2 + c
+
+    pair = device(plane, col, 1 - core)
+    side = device(plane, 1 - col, core)
+    far = [device(p, col, core) for p in place]
+
+    loads = [
+        pltpu.make_async_copy(src.at[0], dst, weight_sem.at[k])
+        for k, (src, dst) in enumerate([(gate_hbm, w_gate), (up_hbm, w_up), (down_hbm, w_down)])
+    ]
+    for load in loads:
+        load.start()
+
+    def block(b):
+        return pl.ds(pl.multiple_of(b * rows, rows), rows)
+
+    held[block(me), :width] = tok_ref[...]
+    lane = lax.broadcasted_iota(jnp.int32, (rows, LANES), 1)
+    row = lax.broadcasted_iota(jnp.int32, (rows, LANES), 0)
+    score = jnp.zeros((rows, LANES), jnp.float32)
+    for k in range(ids_ref.shape[1]):
+        score += jnp.where(ids_ref[:, k : k + 1] == lane % HALF, score_ref[:, k : k + 1], 0.0)
+    score = jnp.where(row < live_ref[0], score, 0.0)
+    high = score.astype(jnp.bfloat16).astype(jnp.float32)
+    held[block(me), width:] = jnp.where(lane < HALF, high, score - high).astype(jnp.bfloat16)
+
+    barrier = pltpu.get_barrier_semaphore()
+    greeted = [pair, side] + far[1:]
+    for other in greeted:
+        pl.semaphore_signal(
+            barrier, inc=1, device_id={"expert": other}, device_id_type=pl.DeviceIdType.MESH
+        )
+    pl.semaphore_wait(barrier, len(greeted))
+
+    sent, pushed = [], []
+
+    def send(src, dst, send_sem, recv_sem, target):
+        copy = pltpu.make_async_remote_copy(
+            src_ref=src, dst_ref=dst, send_sem=send_sem, recv_sem=recv_sem,
+            device_id={"expert": target}, device_id_type=pl.DeviceIdType.MESH,
+        )
+        copy.start()
+        sent.append(copy)
+
+    def arrived(ref, recv_sem):
+        pltpu.make_async_remote_copy(
+            src_ref=ref, dst_ref=ref, send_sem=ag_send.at[0], recv_sem=recv_sem,
+            device_id={"expert": pair}, device_id_type=pl.DeviceIdType.MESH,
+        ).wait_recv()
+
+    def push(b, target):
+        where = held.at[block(b)]
+        send(where, where, ag_send.at[len(pushed)], ag_recv.at[b], target)
+        pushed.append(b)
+
+    def got(b):
+        arrived(held.at[block(b)], ag_recv.at[b])
+
+    def compute(i):
+        here = pl.ds(pl.multiple_of(place[i] * 4 * rows, 4 * rows), 4 * rows)
+        inputs = held[here, :width]
+        gate = jnp.dot(inputs, w_gate[...], preferred_element_type=jnp.float32)
+        up = jnp.dot(inputs, w_up[...], preferred_element_type=jnp.float32)
+        hidden = (gate / (1.0 + jnp.exp(-gate)) * up).astype(jnp.bfloat16)
+        coded = held[here, width:].astype(jnp.float32)
+        lanes = lax.broadcasted_iota(jnp.int32, coded.shape, 1)
+        scale = jnp.sum(jnp.where(lanes % HALF == me // 2, coded, 0.0), axis=1, keepdims=True)
+        if i == 0:
+            loads[2].wait()
+        step = 512 if width % 512 == 0 else width
+        for low in range(0, width, step):
+            cols = pl.ds(low, step)
+            out = jnp.dot(hidden, w_down[:, cols], preferred_element_type=jnp.float32) * scale
+            b00, b01, b10, b11 = [out[k * rows : (k + 1) * rows] for k in range(4)]
+            mine0, theirs0 = jnp.where(core == 0, b00, b01), jnp.where(core == 0, b01, b00)
+            mine1, theirs1 = jnp.where(core == 0, b10, b11), jnp.where(core == 0, b11, b10)
+            kept[i, 0, :, cols] = jnp.where(col == 0, mine0, mine1)
+            kept[i, 1, :, cols] = jnp.where(col == 0, mine1, mine0)
+            to_pair[i, 0, :, cols] = jnp.where(col == 0, theirs0, theirs1).astype(jnp.bfloat16)
+            to_pair[i, 1, :, cols] = jnp.where(col == 0, theirs1, theirs0).astype(jnp.bfloat16)
+        send(to_pair.at[i], from_pair.at[i], pair_send.at[i], pair_recv.at[i], pair)
+
+    def join_pair(i):
+        arrived(from_pair.at[i], pair_recv.at[i])
+        to_side[i] = (kept[i, 1] + from_pair[i, 1].astype(jnp.float32)).astype(jnp.bfloat16)
+        send(to_side.at[i], from_side.at[i], side_send.at[i], side_recv.at[i], side)
+
+    def join_side(i):
+        arrived(from_side.at[i], side_recv.at[i])
+        total = kept[i, 0] + from_pair[i, 0].astype(jnp.float32)
+        return total + from_side[i].astype(jnp.float32)
+
+    def send_far(i):
+        to_far[i] = join_side(i).astype(jnp.bfloat16)
+        send(to_far.at[i], from_far.at[i], far_send.at[i], far_recv.at[i], far[i])
+
+    push(me, side)
+    push(me, pair)
+    for i in range(1, planes):
+        push(me, far[i])
+
+    for i in range(planes):
+        if i + 1 < planes:
+            got(far[i + 1])
+            push(far[i + 1], side)
+            push(far[i + 1], pair)
+        got(device(place[i], 1 - col, core))
+        push(device(place[i], 1 - col, core), pair)
+        got(device(place[i], col, 1 - core))
+        got(device(place[i], 1 - col, 1 - core))
+        if i == 0:
+            loads[0].wait()
+            loads[1].wait()
+        compute(i)
+        if i >= 2:
+            join_pair(i - 1)
+        if i >= 3:
+            send_far(i - 2)
+    if planes > 1:
+        join_pair(planes - 1)
+    join_pair(0)
+    for i in range(max(1, planes - 2), planes):
+        send_far(i)
+    total = join_side(0)
+    for i in range(1, planes):
+        arrived(from_far.at[i], far_recv.at[i])
+        total += from_far[i].astype(jnp.float32)
+    out_ref[...] = total.astype(jnp.bfloat16)
+    for copy in sent:
+        copy.wait_send()
+
+
+def dense_shards(tokens, live_counts, expert_ids, gate_scores, gate_weight, up_weight, down_weight):
+    rows, width = tokens.shape
+    units = gate_weight.shape[2]
+    devices = lax.axis_size("expert")
+    planes = devices // 4
+    block = (rows, width)
+    vmem = pl.BlockSpec(memory_space=pltpu.VMEM)
+    hbm = pl.BlockSpec(memory_space=pl.ANY)
+    dma = pltpu.SemaphoreType.DMA
+    return pl.pallas_call(
+        functools.partial(dense_kernel, planes),
+        out_shape=jax.ShapeDtypeStruct(block, jnp.bfloat16),
+        in_specs=[pl.BlockSpec(memory_space=pltpu.SMEM), vmem, vmem, vmem, hbm, hbm, hbm],
+        out_specs=vmem,
+        scratch_shapes=[
+            pltpu.VMEM((devices * rows, width + LANES), jnp.bfloat16),
+            pltpu.VMEM((width, units), jnp.bfloat16),
+            pltpu.VMEM((width, units), jnp.bfloat16),
+            pltpu.VMEM((units, width), jnp.bfloat16),
+            pltpu.VMEM((planes, 2) + block, jnp.float32),
+            pltpu.VMEM((planes, 2) + block, jnp.bfloat16),
+            pltpu.VMEM((planes, 2) + block, jnp.bfloat16),
+            pltpu.VMEM((planes,) + block, jnp.bfloat16),
+            pltpu.VMEM((planes,) + block, jnp.bfloat16),
+            pltpu.VMEM((planes,) + block, jnp.bfloat16),
+            pltpu.VMEM((planes,) + block, jnp.bfloat16),
+            dma((3,)),
+            dma((4 * planes,)),
+            dma((devices,)),
+            dma((planes,)),
+            dma((planes,)),
+            dma((planes,)),
+            dma((planes,)),
+            dma((planes,)),
+            dma((planes,)),
+        ],
+        compiler_params=pltpu.CompilerParams(
+            collective_id=0, has_side_effects=True, vmem_limit_bytes=60 * 1024 * 1024
+        ),
+    )(live_counts, tokens, expert_ids, gate_scores, gate_weight, up_weight, down_weight)
 
 
 def partner_2(block, axis, apart):
@@ -24,7 +225,7 @@
     return partial_value.reshape(slot_rows.shape)
 
 
-def shards(tokens, live_counts, expert_ids, gate_scores, gate_weight, up_weight, down_weight):
+def packed_shards(tokens, live_counts, expert_ids, gate_scores, gate_weight, up_weight, down_weight):
     tok_dev, model_width = tokens.shape
     top_count = expert_ids.shape[1]
     devices = lax.axis_size("expert")
@@ -70,6 +271,18 @@
     return jnp.where(live_mask[:, None], weighted, jnp.zeros_like(weighted)).astype(jnp.bfloat16)
 
 
+def shards(tokens, live_counts, expert_ids, gate_scores, gate_weight, up_weight, down_weight):
+    args = (tokens, live_counts, expert_ids, gate_scores, gate_weight, up_weight, down_weight)
+    tok_dev, top_count = expert_ids.shape
+    devices = lax.axis_size("expert")
+    experts = devices // 2
+    planes = devices // 4
+    dense = 2 * tok_dev * top_count // experts >= tok_dev
+    if dense and devices % 4 == 0 and planes & (planes - 1) == 0 and experts <= HALF:
+        return dense_shards(*args)
+    return packed_shards(*args)
+
+
 def solution(mesh):
     in_specs = (
         P(("groups", "expert"), None),

time: 82.8 us -> 46.4 us (0.56)
  Pallas kernels: 0 us -> 41.3 us
  waiting for transfers between devices: 30.6 us -> 0 us
  blocking collectives: 28.2 us -> 0 us
  other arithmetic: 8.22 us -> 0 us
  starting transfers between devices: 4.78 us -> 0 us
  matrix products: 3.75 us -> 0 us
  local copies, waits for them, and re-layouts: 5.76 us -> 4.27 us
    pallas_call x0 -> x1, Pallas kernels: none -> 41.3 us  [dense_shards(): pl.pallas_call(functools.partial(dense_kernel, planes), out_shape=jax.Sha...]
    all_to_all x1 -> x0, blocking collectives: 28.2 us -> none  [shards(): lax.all_to_all(outgoing, 'expert', split_axis=0, concat_axis=0, tiled=True)]
    all_to_all x1 -> x0, waiting for transfers between devices: 21.5 us -> none  [shards(): lax.all_to_all(own_part, 'expert', split_axis=0, concat_axis=0, tiled=True)]
    ppermute x2 -> x0, waiting for transfers between devices: 9.08 us -> none  [partner_2(): return lax.ppermute(block, axis, route)]
    all_to_all x1 -> x0, starting transfers between devices: 4.64 us -> none  [shards(): lax.all_to_all(own_part, 'expert', split_axis=0, concat_axis=0, tiled=True)]
    convert_element_type x3 -> x0, other arithmetic: 3.95 us -> none  [the longest x1 3.15 us: shards(): lax.dynamic_slice_in_dim(summed, parity * half_width, half_width, 2)]
    dot_general x4 -> x0, matrix products: 3.75 us -> none  [the longest x1 1.12 us: expert_rows(): jnp.dot(flat_rows, up_weight[0], preferred_element_type=jnp.float32)]
    reshape x1 -> x0, other arithmetic: 2.07 us -> none  [shards(): partial_value = stacked.reshape(devices, capacity, model_width)]
  transfers between devices with their start and end apart: 3 -> 0, of which waited for: 3 -> 0; matrix products, arithmetic and copies ran while one was open for 0% -> 0% of each run, Pallas kernels for 0% -> 0%
where the time goes in v1:
time: 46.4 us; the launch traced here: 46.2 us
  Pallas kernels  41.3 us (89%)
  local copies, waits for them, and re-layouts  4.27 us (9%)
  between operations  0.66 us (1%)
    pallas_call x1, Pallas kernels, dense_shards(): pl.pallas_call(functools.partial(dense_kernel, planes), out_shape=jax.Sha...  41.3 us
    unnamed x3, local copies, waits for them, and re-layouts  4.27 us

profile of v1, /device:TPU:20, one launch (start us, length us, event | category | flops | bytes accessed | tf_op | source)
XLA Modules:
  0.0 46.2 jit_solution(4934922168825594514)
XLA Ops:
  0.7 1.4 %copy.8.ids_ref = s32[16,4]{1,0:T(8,128)} copy(s32[16,4]{0,1:T(4,128)} %param.9) | data formatting | bytes 512 | tf_op args[2]
  2.0 1.4 %copy.9.score_ref = f32[16,4]{1,0:T(8,128)} copy(f32[16,4]{0,1:T(4,128)} %param.10) | data formatting | bytes 512 | tf_op args[3]
  3.4 41.3 %shard_map.73 = bf16[16,3584]{1,0:T(8,128)(2,1)} custom-call(s32[1]{0:T(128)S(6)} %copy.11.live_ref, bf16[16,3584]{1,0:T(8,128)(2,1)} %tok_ref.1, s32[16,4]{1,0:T(8,128)} %copy.8.ids_ref, f32[16,4]{1,0:T(8,128)} %copy.9.score_ref, bf16[1,3584,512]{2,1,0:T(8,128)(2,1)} %gate_hbm.1, bf16[1,3584,512]{2,1,0:T(8,128)(2,1)} %up_hbm.1, bf16[1,512,3584]{2,1,0:T(8,128)(2,1)} %down_hbm.1), custom_call_target="tpu_custom_call" | custom-call | tf_op jit(solution)/shard_map/pallas_call | solution.py:175
  44.7 1.6 %copy.12 = bf16[16,3584]{1,0:T(8,128)(2,1)} copy(bf16[16,3584]{1,0:T(8,128)(2,1)} %shard_map.73) | data formatting | bytes 229376

commit v2 on v1

--- a/solution.py
+++ b/solution.py
@@ -51,8 +51,15 @@
     lane = lax.broadcasted_iota(jnp.int32, (rows, LANES), 1)
     row = lax.broadcasted_iota(jnp.int32, (rows, LANES), 0)
     score = jnp.zeros((rows, LANES), jnp.float32)
-    for k in range(ids_ref.shape[1]):
-        score += jnp.where(ids_ref[:, k : k + 1] == lane % HALF, score_ref[:, k : k + 1], 0.0)
+    across = lax.broadcasted_iota(jnp.int32, (rows, rows), 1)
+    down = lax.broadcasted_iota(jnp.int32, (rows, rows), 0)
+
+    def column(line):
+        return jnp.sum(jnp.where(across == down, line, jnp.zeros_like(line)), axis=1, keepdims=True)
+
+    for k in range(ids_ref.shape[0]):
+        named = column(ids_ref[k : k + 1, :].astype(jnp.float32)).astype(jnp.int32)
+        score += jnp.where(named == lane % HALF, column(score_ref[k : k + 1, :]), 0.0)
     score = jnp.where(row < live_ref[0], score, 0.0)
     high = score.astype(jnp.bfloat16).astype(jnp.float32)
     held[block(me), width:] = jnp.where(lane < HALF, high, score - high).astype(jnp.bfloat16)
@@ -202,7 +209,7 @@
         compiler_params=pltpu.CompilerParams(
             collective_id=0, has_side_effects=True, vmem_limit_bytes=60 * 1024 * 1024
         ),
-    )(live_counts, tokens, expert_ids, gate_scores, gate_weight, up_weight, down_weight)
+    )(live_counts, tokens, expert_ids.T, gate_scores.T, gate_weight, up_weight, down_weight)
 
 
 def partner_2(block, axis, apart):

time: 46.4 us -> 43.7 us (0.942)
  local copies, waits for them, and re-layouts: 4.27 us -> 1.55 us
    unnamed x3 -> x1, local copies, waits for them, and re-layouts: 4.27 us -> 1.55 us
where the time goes in v2:
time: 43.7 us; the launch traced here: 43.5 us
  Pallas kernels  41.3 us (95%)
  local copies, waits for them, and re-layouts  1.55 us (4%)
  between operations  0.66 us (2%)
    pallas_call x1, Pallas kernels, dense_shards(): pl.pallas_call(functools.partial(dense_kernel, planes), out_shape=jax.Sha...  41.3 us
    unnamed x1, local copies, waits for them, and re-layouts  1.55 us

profile of v2, /device:TPU:20, one launch (start us, length us, event | category | flops | bytes accessed | tf_op | source)
XLA Modules:
  0.0 43.5 jit_solution(6389479880383074601)
XLA Ops:
  0.7 41.3 %shard_map.73 = bf16[16,3584]{1,0:T(8,128)(2,1)} custom-call(s32[1]{0:T(128)S(6)} %copy.9.live_ref, bf16[16,3584]{1,0:T(8,128)(2,1)} %tok_ref.1, s32[4,16]{1,0:T(4,128)} %bitcast.2, f32[4,16]{1,0:T(4,128)} %bitcast.3, bf16[1,3584,512]{2,1,0:T(8,128)(2,1)} %gate_hbm.1, bf16[1,3584,512]{2,1,0:T(8,128)(2,1)} %up_hbm.1, bf16[1,512,3584]{2,1,0:T(8,128)(2,1)} %down_hbm.1), custom_call_target="tpu_custom_call" | custom-call | tf_op jit(solution)/shard_map/pallas_call | solution.py:182
  42.0 1.6 %copy.10 = bf16[16,3584]{1,0:T(8,128)(2,1)} copy(bf16[16,3584]{1,0:T(8,128)(2,1)} %shard_map.73) | data formatting | bytes 229376
